TPU v7x, 64 devices: a 2x2x8 block of a 4x4x8 slice. The times are simulated.
64 devices in a mesh: rep: 4 (over x, y), fsdp: 16 (over z, core).
Axes of the slice: x: 2, y: 2, z: 8, core: 2. Of those that a mesh axis runs over, the one named last changes fastest.
The devices are a block of a 4x4x8 slice.
Arguments:
- act_in: bfloat16 [12, 32768, 768], P(None, ('rep', 'fsdp')), parts along dimension 1
- cot_out: bfloat16 [12, 32768, 768], P(None, ('rep', 'fsdp')), parts along dimension 1
- lengths: int32 [12, 64], P(None, ('rep', 'fsdp')), parts along dimension 1
- w_in: bfloat16 [1, 768, 3072], P(None, 'fsdp')
- w_out: bfloat16 [1, 3072, 768], P(None, 'fsdp')
Outputs:
- output 1: float32 [1, 3072, 3072], P(None, ('rep', 'fsdp')), parts along dimension 1
- output 2: float32 [1, 12288, 768], P(None, ('rep', 'fsdp')), parts along dimension 1
There are 4 independent parts. A program takes and returns all parts, laid end to end along the dimension named above; an argument that names none is the same for every part.
All inputs are finite; a program needn't handle non-finite values.
Results may differ from a plain program's by a relative error of at most 0.00938265.
Values are sent between devices in bfloat16 or wider.
A program may use at most 768 MiB of HBM per device.

v0:
```python
import math
import jax
import jax.numpy as jnp
from jax import lax
from jax.sharding import PartitionSpec as P

SQRT_HALF = math.sqrt(0.5)
INV_SQRT_TAU = 1.0 / math.sqrt(2.0 * math.pi)


def gelu_fwd(pre_act):
    return 0.5 * pre_act * (1.0 + lax.erf(pre_act * SQRT_HALF))


def gelu_grad(pre_act):
    return 0.5 * (1.0 + lax.erf(pre_act * SQRT_HALF)) + pre_act * jnp.exp(-0.5 * pre_act * pre_act) * INV_SQRT_TAU


def token_product(left, right):
    return lax.dot_general(left, right, (((0,), (0,)), ((), ())), preferred_element_type=jnp.float32)


def transposed_product(left, right):
    return lax.dot_general(left, right, (((1,), (1,)), ((), ())), preferred_element_type=jnp.float32)


def gather_rows(shard):
    return lax.all_gather(shard, 'fsdp', axis=0, tiled=True)


def scatter_rows(full_grad):
    return lax.psum_scatter(full_grad, 'fsdp', scatter_dimension=0, tiled=True)


def solution(mesh):
    shard_spec = P(None, ('rep', 'fsdp'), None)
    len_spec = P(None, ('rep', 'fsdp'))
    weight_spec = P(None, 'fsdp', None)

    def local_step(act_in, cot_out, lengths, w_in, w_out):
        micro_count, tok_count, model_width = act_in.shape
        layer_count = w_in.shape[0]
        keep_mask = jnp.arange(tok_count)[None, :] < lengths
        cot_cur = jnp.where(keep_mask[:, :, None], cot_out, jnp.zeros_like(cot_out)).reshape(micro_count * tok_count, model_width)
        hidden = act_in.reshape(micro_count * tok_count, model_width)
        saved_acts = []
        for layer_idx in range(layer_count):
            w_up = gather_rows(w_in[layer_idx])
            pre_act = jnp.dot(hidden, w_up, preferred_element_type=jnp.float32).astype(jnp.bfloat16)
            post_act = gelu_fwd(pre_act.astype(jnp.float32)).astype(jnp.bfloat16)
            saved_acts.append((hidden, pre_act, post_act))
            if layer_idx < layer_count - 1:
                w_down = gather_rows(w_out[layer_idx])
                hidden = (hidden.astype(jnp.float32) + jnp.dot(post_act, w_down, preferred_element_type=jnp.float32)).astype(jnp.bfloat16)
        grads_in = [None] * layer_count
        grads_out = [None] * layer_count
        for layer_idx in reversed(range(layer_count)):
            hidden, pre_act, post_act = saved_acts[layer_idx]
            if layer_idx < layer_count - 1:
                w_up = gather_rows(w_in[layer_idx])
            w_down = gather_rows(w_out[layer_idx])
            grads_out[layer_idx] = scatter_rows(token_product(post_act, cot_cur))
            d_act = transposed_product(cot_cur, w_down)
            d_pre = (d_act * gelu_grad(pre_act.astype(jnp.float32))).astype(jnp.bfloat16)
            grads_in[layer_idx] = scatter_rows(token_product(hidden, d_pre))
            if layer_idx > 0:
                cot_cur = (cot_cur.astype(jnp.float32) + transposed_product(d_pre, w_up)).astype(jnp.bfloat16)
        return jnp.stack(grads_in), jnp.stack(grads_out)

    return jax.shard_map(local_step, mesh=mesh, in_specs=(shard_spec, shard_spec, len_spec, weight_spec, weight_spec), out_specs=(shard_spec, shard_spec), check_vma=False)
```

profile of v0, /device:TPU:21, one launch (start us, length us, event | category | flops | bytes accessed | tf_op | source)
XLA Modules:
  0.0 339.4 jit_solution(15027220554161922217)
XLA Ops:
  7.2 0.1 all-gather.7.cloned.1.call-start
  7.2 0.7 all-gather.7.cloned.1.call-update
  8.0 0.1 all-gather.5.cloned.1.call-start
  8.0 0.7 all-gather.5.cloned.1.call-update
  8.8 0.1 reduce-scatter.7.cloned.1.call-start
  8.8 0.7 iota_compare_fusion
  9.6 9.5 %broadcast_select_fusion = bf16[12,512,768]{2,1,0:T(8,128)(2,1)} fusion(bf16[12,512,768]{2,1,0:T(8,128)(2,1)} %param.6, pred[12,512]{1,0:T(8,128)(4,1)S(1)} %iota_compare_fusion), kind=kLoop, calls=%fused_computation.17 | loop fusion | flops 4718592 | bytes 18880512 | tf_op jit(solution)/shard_map/jit(_where)/select_n | solution.py:44
  19.1 34.6 %all-gather.7.cloned.1.call-done = bf16[1,768,3072]{2,1,0:T(8,128)(2,1)} async-done(((bf16[1,48,3072]{2,1,0:T(8,128)(2,1)}), bf16[1,768,3072]{2,1,0:T(8,128)(2,1)}) %all-gather.7.cloned.1.call-update) | async-done | bytes 4718608 | tf_op jit(solution)/shard_map/all_gather | solution.py:28
  53.7 36.9 %convolution_convert_fusion = bf16[6144,3072]{1,0:T(8,128)(2,1)} fusion(bf16[6144,768]{1,0:T(8,128)(2,1)} %bitcast.34, bf16[1,768,3072]{2,1,0:T(8,128)(2,1)} %all-gather.7.cloned.1.call-done), kind=kOutput, calls=%fused_computation.16 | convolution fusion | flops 29009903616 | bytes 51904512 | tf_op jit(solution)/shard_map/dot_general | solution.py:49
  90.6 2.6 all-gather.5.cloned.1.call-done
  93.2 54.5 %fusion.6.clone.4 = bf16[6144,3072]{1,0:T(8,128)(2,1)} fusion(bf16[6144,3072]{1,0:T(8,128)(2,1)} %convolution_convert_fusion, bf16[6144,768]{1,0:T(8,128)(2,1)} %bitcast.30, bf16[1,3072,768]{2,1,0:T(8,128)(2,1)} %all-gather.5.cloned.1.call-done), kind=kOutput, calls=%fused_computation.11.clone.clone.clone.1 | convolution fusion | flops 29198647296 | bytes 89653248 | tf_op jit(solution)/shard_map/dot_general | solution.py:24
  147.7 38.6 %convolution_bitcast_fusion = f32[768,3072]{0,1:T(8,128)} fusion(bf16[6144,768]{1,0:T(8,128)(2,1)} %bitcast.35, bf16[6144,3072]{1,0:T(8,128)(2,1)} %fusion.6.clone.4), kind=kOutput, calls=%fused_computation.18 | convolution fusion | flops 28991029248 | bytes 56623104 | tf_op jit(solution)/shard_map/dot_general | solution.py:20
  186.3 9.6 %copy.9 = f32[768,3072]{1,0:T(8,128)} copy(f32[768,3072]{0,1:T(8,128)} %convolution_bitcast_fusion) | data formatting | bytes 18874368
  195.9 0.1 reduce-scatter.7.cloned.1.call-update
  196.0 0.1 reduce-scatter.5.cloned.1.call-start
  196.1 41.3 %fusion.9 = f32[3072,768]{1,0:T(8,128)} fusion(bf16[6144,768]{1,0:T(8,128)(2,1)} %bitcast.31, bf16[6144,3072]{1,0:T(8,128)(2,1)} %convolution_convert_fusion), kind=kOutput, calls=%fused_computation.14 | convolution fusion | flops 29104275456 | bytes 56623104 | tf_op jit(solution)/shard_map/dot_general | solution.py:20
  237.4 0.1 reduce-scatter.5.cloned.1.call-update
  237.5 24.0 %reduce-scatter.7.cloned.1.call-done = f32[48,3072]{1,0:T(8,128)} async-done(((f32[768,3072]{1,0:T(8,128)}), f32[48,3072]{1,0:T(8,128)}) %reduce-scatter.7.cloned.1.call-update) | async-done | bytes 589840
  261.4 1.5 copy.10
  263.0 1.3 copy.8
  264.2 68.6 %reduce-scatter.5.cloned.1.call-done = f32[192,768]{1,0:T(8,128)} async-done(((f32[3072,768]{1,0:T(8,128)}), f32[192,768]{1,0:T(8,128)}) %reduce-scatter.5.cloned.1.call-update) | async-done | bytes 589840 | tf_op jit(solution)/shard_map/reduce_scatter | solution.py:32
Async XLA Ops:
  7.2 46.5 %all-gather.7.cloned.1.call-start = ((), (), s32[]{:S(2)}) async-start(), calls=%async_computation.4 | async-start | bytes 5013504 | tf_op jit(solution)/shard_map/all_gather | solution.py:28
  8.0 85.2 %all-gather.5.cloned.1.call-start = ((), (), s32[]{:S(2)}) async-start(), calls=%async_computation.3 | async-start | bytes 5013504 | tf_op jit(solution)/shard_map/all_gather | solution.py:28
  8.8 252.6 %reduce-scatter.7.cloned.1.call-start = ((), (), s32[]{:S(2)}) async-start(), calls=%async_computation.5 | async-start | bytes 10027008
  196.0 136.8 %reduce-scatter.5.cloned.1.call-start = ((), (), s32[]{:S(2)}) async-start(), calls=%async_computation.2 | async-start | bytes 10027008 | tf_op jit(solution)/shard_map/reduce_scatter | solution.py:32
Sparse Core Ops, SparseCore 0:
  9.6 44.0 all-gather.6
  55.3 37.7 all-gather.4
  196.1 65.2 reduce-scatter.6
  264.2 68.5 reduce-scatter.4
where the time goes:
time: 342 us; the launch traced here: 339 us
  matrix products  171 us (50%)
  waiting for transfers between devices  131 us (38%)
  between operations  13.8 us (4%)
  local copies, waits for them, and re-layouts  12.4 us (4%)
  other arithmetic  10.2 us (3%)
    dot_general x2, matrix products, token_product(): lax.dot_general(left, right, (((0,), (0,)), ((), ())), preferred_element_...  79.9 us
    reduce_scatter x1, waiting for transfers between devices, scatter_rows(): return lax.psum_scatter(full_grad, 'fsdp', scatter_dimension=0, tiled=True)  68.6 us
    dot_general x1, matrix products, transposed_product(): lax.dot_general(left, right, (((1,), (1,)), ((), ())), preferred_element_...  54.5 us
    all_gather x2, waiting for transfers between devices, gather_rows(): return lax.all_gather(shard, 'fsdp', axis=0, tiled=True)  37.2 us
    dot_general x1, matrix products, local_step(): jnp.dot(hidden, w_up, preferred_element_type=jnp.float32)  36.9 us
    unnamed x5, waiting for transfers between devices  25.5 us
    unnamed x3, local copies, waits for them, and re-layouts  12.4 us
    select_n x1, other arithmetic, local_step(): jnp.where(keep_mask[:, :, None], cot_out, jnp.zeros_like(cot_out))  9.5 us
  transfers between devices with their start and end apart: 4, of which 4 were waited for; matrix products, arithmetic and copies ran while one was open for 27% of the time, Pallas kernels for 0%

commit v1 on v0

v1 whole, which is shorter than its diff:
```python
import functools
import math
import jax
import jax.numpy as jnp
from jax import lax
from jax.experimental import pallas as pl
from jax.experimental.pallas import tpu as pltpu
from jax.sharding import PartitionSpec as P

SQRT_HALF = math.sqrt(0.5)
INV_SQRT_TAU = 1.0 / math.sqrt(2.0 * math.pi)
F32 = jnp.float32
BF16 = jnp.bfloat16
MESH = pl.DeviceIdType.MESH
NT_DIMS = (((1,), (1,)), ((), ()))

SLICE = 256
LANES = 2
HEAD = 3
LONG, SHORT = 4, 3


def gelu_pair(pre_act):
    cdf = 0.5 * (1.0 + lax.erf(pre_act * SQRT_HALF))
    return pre_act * cdf, cdf + pre_act * jnp.exp(-0.5 * pre_act * pre_act) * INV_SQRT_TAU


def dot_nt(left, right):
    return lax.dot_general(left, right, NT_DIMS, preferred_element_type=F32)


def dot_nn(left, right):
    return jnp.dot(left, right, preferred_element_type=F32)


def step_kernel(cfg, act_hbm, cot_hbm, len_smem, wts_hbm, out_hbm,
                act_t, cot, stage, wts, up_t, down, acc, post_s, dpre_s,
                peer, ring_in, ring_out, fin,
                load_sem, agl_s, agl_r, ags_s, ags_r, agx_s, agx_r,
                ex_s, ex_r, rl_s, rl_r, rs_s, rs_r, fin_s, fin_r):
    n_slice, n_dev, micro, toks, width, tiles = cfg
    n_chip = n_dev // 2
    per_dev = SLICE_OF(cfg) // n_dev
    n_blk = width // SLICE_OF(cfg)
    rows_dev = width // n_dev
    chunk = 2 * per_dev
    dev = lax.axis_index('fsdp')
    chip = dev // 2
    core = dev % 2
    sgn = 1 - 2 * core

    def at_chip(off):
        return (chip + sgn * off + 2 * n_chip) % n_chip

    nxt = at_chip(1) * 2 + core
    prv = at_chip(-1) * 2 + core
    sib = chip * 2 + 1 - core

    def remote(src, dst, send, recv, target):
        return pltpu.make_async_remote_copy(src_ref=src, dst_ref=dst, send_sem=send, recv_sem=recv,
                                            device_id={'fsdp': target}, device_id_type=MESH)

    barrier = pltpu.get_barrier_semaphore()
    for other in (nxt, prv, sib):
        pl.semaphore_signal(barrier, inc=1, device_id={'fsdp': other}, device_id_type=MESH)

    own_load = pltpu.make_async_copy(wts_hbm, wts.at[:, dev], load_sem.at[2 * micro])
    own_load.start()

    def act_load(k):
        return pltpu.make_async_copy(act_hbm.at[k], stage.at[k % 4], load_sem.at[k])

    def cot_load(k):
        return pltpu.make_async_copy(cot_hbm.at[k], cot.at[k // LANES, pl.ds((k % LANES) * toks, toks)],
                                     load_sem.at[micro + k])

    for k in range(4):
        act_load(k).start()
        cot_load(k).start()
    own_load.wait()
    pl.semaphore_wait(barrier, 3)

    def piece(q, off):
        return wts.at[q, at_chip(off) * 2 + core]

    def ag_long(q, t):
        ref = piece(q, 1 - t)
        return remote(ref, ref, agl_s.at[q, t - 1], agl_r.at[q, t - 1], nxt)

    def ag_short(q, t):
        ref = piece(q, t - 1)
        return remote(ref, ref, ags_s.at[q, t - 1], ags_r.at[q, t - 1], prv)

    def ag_sib(q, idx, off):
        ref = piece(q, off)
        return remote(ref, ref, agx_s.at[q, idx], agx_r.at[q, idx], sib)

    def ag_first(q):
        ag_long(q, 1).start()
        ag_short(q, 1).start()
        ag_sib(q, 0, 0).start()

    def ag_mid(q, t):
        ag_long(q, t - 1).wait_recv()
        ag_long(q, t).start()
        ag_sib(q, t - 1, 1 - t).start()
        ag_short(q, t - 1).wait_recv()

        @pl.when(t <= SHORT)
        def _():
            ag_short(q, t).start()
        ag_sib(q, LONG + t - 1, t - 1).start()

    def ag_last(q):
        ag_long(q, LONG).wait_recv()
        ag_sib(q, LONG, -LONG).start()

    def ag_finish(q):
        for idx in range(LONG + SHORT + 1):
            ag_sib(q, idx, 0).wait_recv()
        for idx in range(LONG + SHORT + 1):
            ag_sib(q, idx, 0).wait_send()
        for t in range(1, LONG + 1):
            ag_long(q, t).wait_send()
        for t in range(1, SHORT + 1):
            ag_short(q, t).wait_send()

    def load_tile(k):
        act_load(k).wait()
        act_t[k // LANES, :, (k % LANES) * toks:(k % LANES + 1) * toks] = stage[k % 4].T
        cot_load(k).wait()
        row = lax.broadcasted_iota(jnp.int32, (toks, 1), 0)
        rows = pl.ds((k % LANES) * toks, toks)
        val = cot[k // LANES, rows, :]
        cot[k // LANES, rows, :] = jnp.where(row < len_smem[k, 0], val, jnp.zeros_like(val))
        if k + 4 < micro:
            act_load(k + 4).start()
            cot_load(k + 4).start()

    for q in range(HEAD):
        ag_first(q)
    per_tick = micro // LONG
    for t in range(2, LONG + 2):
        for k in range((t - 2) * per_tick, (t - 1) * per_tick):
            load_tile(k)
        for q in range(HEAD):
            if t <= LONG:
                ag_mid(q, t)
            else:
                ag_last(q)

    def exchange(q):
        return remote(acc.at[q % 4, 1 - core], peer.at[q % 3], ex_s.at[q % 3], ex_r.at[q % 3], sib)

    def send_long(q, t):
        return remote(ring_out.at[q % 3, t - 1], ring_in.at[q % 3, t - 1],
                      rl_s.at[q % 3, t - 1], rl_r.at[q % 3, t - 1], nxt)

    def send_short(q, t):
        return remote(ring_out.at[q % 3, LONG + t - 1], ring_in.at[q % 3, LONG + t - 1],
                      rs_s.at[q % 3, t - 1], rs_r.at[q % 3, t - 1], prv)

    def own_sum(q, off):
        rows = pl.ds(pl.multiple_of(at_chip(off) * chunk, chunk), chunk)
        return acc[q % 4, core, rows, :] + peer[q % 3, rows, :]

    def send_fin(q):
        return remote(ring_out.at[q % 3, LONG + SHORT, pl.ds(pl.multiple_of((1 - core) * per_dev, per_dev), per_dev)],
                      fin.at[core, q], fin_s.at[q], fin_r.at[q], sib)

    def rs_exchange(q):
        @pl.when(q >= 3)
        def _():
            send_fin(q - 3).wait_recv()
        exchange(q).start()

    def rs_round(q, t):
        if t == 1:
            exchange(q).wait_recv()
        val = own_sum(q, 5 - t)
        if t > 1:
            send_long(q, t - 1).wait_recv()
            val = val + ring_in[q % 3, t - 2]
        ring_out[q % 3, t - 1] = val
        if t <= SHORT:
            val = own_sum(q, t - 4)
            if t > 1:
                send_short(q, t - 1).wait_recv()
                val = val + ring_in[q % 3, LONG + t - 2]
            ring_out[q % 3, LONG + t - 1] = val
        send_long(q, t).start()
        if t <= SHORT:
            send_short(q, t).start()

    def rs_final(q):
        val = own_sum(q, 0)
        send_long(q, LONG).wait_recv()
        send_short(q, SHORT).wait_recv()
        val = val + ring_in[q % 3, LONG - 1] + ring_in[q % 3, LONG + SHORT - 1]
        ring_out[q % 3, LONG + SHORT] = val
        send_fin(q).start()
        mine = pl.ds(pl.multiple_of(core * per_dev, per_dev), per_dev)
        fin[core, q] = ring_out[q % 3, LONG + SHORT, mine]
        exchange(q).wait_send()
        for t in range(1, LONG + 1):
            send_long(q, t).wait_send()
        for t in range(1, SHORT + 1):
            send_short(q, t).wait_send()
        send_fin(q).wait_send()

    def guarded(q, fn):
        @pl.when(jnp.logical_and(q >= 0, q < n_slice))
        def _():
            fn(q)

    def comm(s, t):
        @pl.when(t == 0)
        def _():
            guarded(s - 1, rs_exchange)

        @pl.when(t == 1 % tiles)
        def _():
            guarded(s - 1, lambda q: rs_round(q, 1))

        @pl.when(t == 2 % tiles)
        def _():
            guarded(s - 2, lambda q: rs_round(q, 3))
            guarded(s - 3, rs_final)

        @pl.when(t == 4 % tiles)
        def _():
            guarded(s - 1, lambda q: rs_round(q, 2))

        @pl.when(t == 5 % tiles)
        def _():
            guarded(s - 2, lambda q: rs_round(q, 4))

    def gather(n):
        half = n // 2
        q2 = 2 * HEAD + (half - 4) // 4
        t2 = (half + 4) % 4 + 1

        @pl.when(n == 0)
        def _():
            for q in range(HEAD, 2 * HEAD):
                ag_first(q)

        @pl.when(jnp.logical_and(half >= 1, half <= 3))
        def _():
            for q in range(HEAD, 2 * HEAD):
                ag_mid(q, half + 1)

        @pl.when(half == 4)
        def _():
            for q in range(HEAD, 2 * HEAD):
                ag_last(q)

        @pl.when(jnp.logical_and(half >= 4, q2 < n_slice))
        def _():
            @pl.when(t2 == 1)
            def _():
                ag_first(q2)

            @pl.when(t2 > 1)
            def _():
                ag_mid(q2, t2)

        @pl.when(jnp.logical_and(jnp.logical_and(half >= 8, t2 == 1), q2 <= n_slice))
        def _():
            ag_last(q2 - 1)

    def main(n, carry):
        s = n // tiles
        t = n % tiles

        @pl.when(t == 0)
        def _():
            ag_finish(s)
            up_t[...] = wts[s, :, 0:rows_dev, :].reshape(width, n_dev * per_dev).T
            for b in range(n_blk):
                lo = rows_dev + b * per_dev
                down[:, b * n_dev * per_dev:(b + 1) * n_dev * per_dev] = (
                    wts[s, :, lo:lo + per_dev, :].reshape(n_dev * per_dev, n_dev * per_dev))
            acc[s % 4] = jnp.zeros((2, n_dev * per_dev, width), F32)

        pre = dot_nn(up_t[...], act_t[t]).astype(BF16).astype(F32)
        post, slope = gelu_pair(pre)
        d_act = dot_nt(down[...], cot[t])
        post_s[...] = post.astype(BF16)
        dpre_s[...] = (d_act * slope).astype(BF16)
        acc[s % 4, 0] += dot_nn(post_s[...], cot[t])
        g_in = dot_nt(act_t[t], dpre_s[...])
        for d in range(n_dev):
            for b in range(n_blk):
                lo = d * rows_dev + b * per_dev
                acc[s % 4, 1, d * per_dev:(d + 1) * per_dev, b * n_dev * per_dev:(b + 1) * n_dev * per_dev] += (
                    g_in[lo:lo + per_dev])

        @pl.when(n % 2 == 0)
        def _():
            gather(n)
        comm(s, t)
        return carry

    lax.fori_loop(0, n_slice * tiles, main, 0)

    def tail(n, carry):
        comm(n // tiles, n % tiles)
        return carry

    lax.fori_loop(n_slice * tiles, (n_slice + 2) * tiles + 3, tail, 0)
    for q in range(n_slice - 3, n_slice):
        send_fin(q).wait_recv()
    done = pltpu.make_async_copy(fin, out_hbm, load_sem.at[0])
    done.start()
    done.wait()


def SLICE_OF(cfg):
    return min(SLICE, cfg[4] // 3)


def run_step(n_dev, act, cot, lengths, w_in, w_out):
    micro, toks, width = act.shape
    hidden = w_in.shape[1]
    sl = min(SLICE, width // 3)
    n_slice, per_dev, n_blk, rows_dev = hidden // sl, sl // n_dev, width // sl, width // n_dev
    tiles = micro // LANES
    cfg = (n_slice, n_dev, micro, toks, width, tiles)
    up = w_in.reshape(rows_dev, n_dev, n_slice, per_dev).transpose(2, 0, 1, 3).reshape(n_slice, rows_dev, sl)
    down = w_out.reshape(n_slice, per_dev, n_blk, sl).transpose(0, 2, 1, 3).reshape(n_slice, rows_dev, sl)
    wts = jnp.concatenate([up, down], axis=1)
    hbm = pl.BlockSpec(memory_space=pl.ANY)
    dma = pltpu.SemaphoreType.DMA
    chunk = 2 * per_dev
    tok = toks * LANES
    out = pl.pallas_call(
        functools.partial(step_kernel, cfg),
        name='mlp_grads',
        out_shape=jax.ShapeDtypeStruct((2, n_slice, per_dev, width), F32),
        in_specs=[hbm, hbm, pl.BlockSpec(memory_space=pltpu.SMEM), hbm],
        out_specs=hbm,
        scratch_shapes=[
            pltpu.VMEM((tiles, width, tok), BF16),
            pltpu.VMEM((tiles, tok, width), BF16),
            pltpu.VMEM((4, toks, width), BF16),
            pltpu.VMEM((n_slice, n_dev, 2 * rows_dev, sl), BF16),
            pltpu.VMEM((sl, width), BF16),
            pltpu.VMEM((sl, width), BF16),
            pltpu.VMEM((4, 2, sl, width), F32),
            pltpu.VMEM((sl, tok), BF16),
            pltpu.VMEM((sl, tok), BF16),
            pltpu.VMEM((3, sl, width), F32),
            pltpu.VMEM((3, LONG + SHORT, chunk, width), F32),
            pltpu.VMEM((3, LONG + SHORT + 1, chunk, width), F32),
            pltpu.VMEM((2, n_slice, per_dev, width), F32),
            dma((2 * micro + 1,)),
            dma((n_slice, LONG)), dma((n_slice, LONG)), dma((n_slice, SHORT)), dma((n_slice, SHORT)),
            dma((n_slice, LONG + SHORT + 1)), dma((n_slice, LONG + SHORT + 1)),
            dma((3,)), dma((3,)), dma((3, LONG)), dma((3, LONG)), dma((3, SHORT)), dma((3, SHORT)),
            dma((n_slice,)), dma((n_slice,)),
        ],
        compiler_params=pltpu.CompilerParams(collective_id=0, has_side_effects=True, vmem_limit_bytes=62 * 2 ** 20),
    )(act, cot, lengths, wts)
    grad_out = out[0].reshape(n_slice * per_dev, width)
    grad_in = out[1].reshape(n_slice, per_dev, n_blk, n_dev, per_dev).transpose(2, 1, 3, 0, 4)
    return grad_in.reshape(rows_dev, hidden), grad_out


def solution(mesh):
    n_dev = mesh.shape['fsdp']
    shard_spec = P(None, ('rep', 'fsdp'), None)
    len_spec = P(None, ('rep', 'fsdp'))
    weight_spec = P(None, 'fsdp', None)

    def local_step(act_in, cot_out, lengths, w_in, w_out):
        grad_in, grad_out = run_step(n_dev, act_in, cot_out, lengths, w_in[0], w_out[0])
        return grad_in[None], grad_out[None]

    return jax.shard_map(local_step, mesh=mesh, in_specs=(shard_spec, shard_spec, len_spec, weight_spec, weight_spec),
                         out_specs=(shard_spec, shard_spec), check_vma=False)
```

time: 342 us -> 235 us (0.69)
  Pallas kernels: 0 us -> 212 us
  matrix products: 171 us -> 0 us
  waiting for transfers between devices: 131 us -> 0 us
  between operations: 13.8 us -> 0.69 us
  other arithmetic: 10.2 us -> 0.87 us
  local copies, waits for them, and re-layouts: 12.4 us -> 21.6 us
    pallas_call x0 -> x1, Pallas kernels: none -> 212 us  [run_step(): pl.pallas_call(functools.partial(step_kernel, cfg), name='mlp_grads', out...]
    dot_general x4 -> x0, matrix products: 171 us -> none  [the longest x2 79.9 us: token_product(): lax.dot_general(left, right, (((0,), (0,)), ((), ())), preferred_element_...]
    reduce_scatter x1 -> x0, waiting for transfers between devices: 68.6 us -> none  [scatter_rows(): return lax.psum_scatter(full_grad, 'fsdp', scatter_dimension=0, tiled=True)]
    all_gather x2 -> x0, waiting for transfers between devices: 37.2 us -> none  [gather_rows(): return lax.all_gather(shard, 'fsdp', axis=0, tiled=True)]
    unnamed x5 -> x0, waiting for transfers between devices: 25.5 us -> none
    another operation x0 -> x4, local copies, waits for them, and re-layouts: none -> 17.2 us  [the longest x2 10.8 us: run_step(): out[1].reshape(n_slice, per_dev, n_blk, n_dev, per_dev)]
    unnamed x3 -> x4, local copies, waits for them, and re-layouts: 12.4 us -> 1.76 us
    select_n x1 -> x0, other arithmetic: 9.5 us -> none  [local_step(): jnp.where(keep_mask[:, :, None], cot_out, jnp.zeros_like(cot_out))]
  transfers between devices with their start and end apart: 4 -> 0, of which waited for: 4 -> 0; matrix products, arithmetic and copies ran while one was open for 27% -> 0% of each run, Pallas kernels for 0% -> 0%
where the time goes in v1:
time: 235 us
  Pallas kernels  212 us (90%)
  local copies, waits for them, and re-layouts  21.6 us (9%)
    pallas_call x1, Pallas kernels, run_step(): pl.pallas_call(functools.partial(step_kernel, cfg), name='mlp_grads', out...  212 us
    another operation x2, local copies, waits for them, and re-layouts, run_step(): out[1].reshape(n_slice, per_dev, n_blk, n_dev, per_dev)  10.8 us
    another operation x1, local copies, waits for them, and re-layouts, local_step(): return (grad_in[None], grad_out[None])  5.29 us

profile of v1, /device:TPU:21, one launch (start us, length us, event | category | flops | bytes accessed | tf_op | source)
XLA Modules:
  0.0 235.0 jit_solution(8132218304807302608)
XLA Ops:
  0.6 0.0 copy-start
  0.6 1.4 copy.15.len_smem
  2.0 1.1 reshape_squeeze.10
  3.2 0.0 copy-done
  3.2 0.4 copy.11
  3.5 0.2 copy.12
  3.7 0.3 copy.14
  4.0 0.9 pad_maximum_fusion.wts_hbm
  4.9 211.9 %mlp_grads.1 = f32[2,12,16,768]{3,2,1,0:T(8,128)} custom-call(bf16[12,512,768]{2,1,0:T(8,128)(2,1)} %act_hbm.1, bf16[12,512,768]{2,1,0:T(8,128)(2,1)} %cot_hbm.1, s32[12,1]{1,0:T(8,128)} %copy.15.len_smem, bf16[12,96,256]{2,1,0:T(8,128)(2,1)} %pad_maximum_fusion.wts_hbm), custom_call_target="tpu_custom_call" | custom-call | tf_op jit(solution)/shard_map/mlp_grads/pallas_call | solution.py:337
  216.7 2.1 fusion
  218.9 3.0 %reshape_squeeze.11 = f32[12,16,3,16,16]{4,3,2,1,0:T(8,128)} reshape(f32[1,12,16,768]{3,2,1,0:T(8,128)S(1)} %get-tuple-element.3) | data formatting | bytes 1179648 | tf_op jit(solution)/shard_map/reshape;squeeze | solution.py:366
  221.9 7.8 %copy.18 = f32[12,16,3,16,16]{4,0,3,1,2:T(8,128)} copy(f32[12,16,3,16,16]{4,3,2,1,0:T(8,128)} %reshape_squeeze.11) | data formatting | bytes 1179648 | tf_op jit(solution)/shard_map/reshape;squeeze | solution.py:366
  229.7 5.3 %broadcast_in_dim_reshape.3 = f32[1,48,3072]{2,1,0:T(8,128)} reshape(f32[3,16,16,12,16]{4,3,2,1,0:T(8,128)} %bitcast.12) | data formatting | bytes 1179648 | tf_op jit(solution)/shard_map/broadcast_in_dim;reshape | solution.py:378
  (1 shorter events, 0.0 us)
Async XLA Ops:
  0.6 2.5 %copy-start = (bf16[1,48,3072]{2,1,0:T(8,128)(2,1)S(1)}, bf16[1,48,3072]{2,1,0:T(8,128)(2,1)}, u32[]{:S(2)}) copy-start(bf16[1,48,3072]{2,1,0:T(8,128)(2,1)} %param.8) | copy-start | bytes 884740

commit v2 on v1

--- a/solution.py
+++ b/solution.py
@@ -33,9 +33,9 @@
     return jnp.dot(left, right, preferred_element_type=F32)
 
 
-def step_kernel(cfg, act_hbm, cot_hbm, len_smem, wts_hbm, out_hbm,
+def step_kernel(cfg, act_hbm, cot_hbm, len_smem, up_hbm, down_hbm, gin_hbm, gout_hbm,
                 act_t, cot, stage, wts, up_t, down, acc, post_s, dpre_s,
-                peer, ring_in, ring_out, fin,
+                peer, ring_in, ring_out, fin, gin,
                 load_sem, agl_s, agl_r, ags_s, ags_r, agx_s, agx_r,
                 ex_s, ex_r, rl_s, rl_r, rs_s, rs_r, fin_s, fin_r):
     n_slice, n_dev, micro, toks, width, tiles = cfg
@@ -64,8 +64,14 @@
     for other in (nxt, prv, sib):
         pl.semaphore_signal(barrier, inc=1, device_id={'fsdp': other}, device_id_type=MESH)
 
-    own_load = pltpu.make_async_copy(wts_hbm, wts.at[:, dev], load_sem.at[2 * micro])
-    own_load.start()
+    sl = n_dev * per_dev
+    own_loads = [pltpu.make_async_copy(up_hbm, wts.at[:, dev, pl.ds(0, rows_dev)], load_sem.at[2 * micro])]
+    for b in range(n_blk):
+        own_loads.append(pltpu.make_async_copy(down_hbm.at[:, :, pl.ds(b * sl, sl)],
+                                               wts.at[:, dev, pl.ds(rows_dev + b * per_dev, per_dev)],
+                                               load_sem.at[2 * micro + 1 + b]))
+    for copy in own_loads:
+        copy.start()
 
     def act_load(k):
         return pltpu.make_async_copy(act_hbm.at[k], stage.at[k % 4], load_sem.at[k])
@@ -77,8 +83,10 @@
     for k in range(4):
         act_load(k).start()
         cot_load(k).start()
-    own_load.wait()
-    pl.semaphore_wait(barrier, 3)
+    for copy in own_loads:
+        copy.wait()
+    with jax.named_scope('bar'):
+        pl.semaphore_wait(barrier, 3)
 
     def piece(q, off):
         return wts.at[q, at_chip(off) * 2 + core]
@@ -106,8 +114,7 @@
         ag_sib(q, t - 1, 1 - t).start()
         ag_short(q, t - 1).wait_recv()
 
-        @pl.when(t <= SHORT)
-        def _():
+        if t <= SHORT:
             ag_short(q, t).start()
         ag_sib(q, LONG + t - 1, t - 1).start()
 
@@ -132,22 +139,29 @@
         row = lax.broadcasted_iota(jnp.int32, (toks, 1), 0)
         rows = pl.ds((k % LANES) * toks, toks)
         val = cot[k // LANES, rows, :]
-        cot[k // LANES, rows, :] = jnp.where(row < len_smem[k, 0], val, jnp.zeros_like(val))
+        cot[k // LANES, rows, :] = jnp.where(row < len_smem[k], val, jnp.zeros_like(val))
         if k + 4 < micro:
             act_load(k + 4).start()
             cot_load(k + 4).start()
 
-    for q in range(HEAD):
-        ag_first(q)
+    def ag_step(q, t):
+        if t == 1:
+            ag_first(q)
+        elif t <= LONG:
+            ag_mid(q, t)
+        else:
+            ag_last(q)
+
+    ag_step(0, 1)
     per_tick = micro // LONG
-    for t in range(2, LONG + 2):
-        for k in range((t - 2) * per_tick, (t - 1) * per_tick):
-            load_tile(k)
-        for q in range(HEAD):
-            if t <= LONG:
-                ag_mid(q, t)
-            else:
-                ag_last(q)
+    for tick in range(2, LONG + 2):
+        with jax.named_scope(f'load{tick}'):
+            for k in range((tick - 2) * per_tick, (tick - 1) * per_tick):
+                load_tile(k)
+        with jax.named_scope(f'head{tick}'):
+            for q in range(HEAD):
+                if tick - q >= 1:
+                    ag_step(q, tick - q)
 
     def exchange(q):
         return remote(acc.at[q % 4, 1 - core], peer.at[q % 3], ex_s.at[q % 3], ex_r.at[q % 3], sib)
@@ -172,6 +186,7 @@
         @pl.when(q >= 3)
         def _():
             send_fin(q - 3).wait_recv()
+            send_fin(q - 3).wait_send()
         exchange(q).start()
 
     def rs_round(q, t):
@@ -206,68 +221,46 @@
             send_long(q, t).wait_send()
         for t in range(1, SHORT + 1):
             send_short(q, t).wait_send()
-        send_fin(q).wait_send()
-
-    def guarded(q, fn):
-        @pl.when(jnp.logical_and(q >= 0, q < n_slice))
-        def _():
-            fn(q)
-
-    def comm(s, t):
-        @pl.when(t == 0)
-        def _():
-            guarded(s - 1, rs_exchange)
-
-        @pl.when(t == 1 % tiles)
-        def _():
-            guarded(s - 1, lambda q: rs_round(q, 1))
-
-        @pl.when(t == 2 % tiles)
-        def _():
-            guarded(s - 2, lambda q: rs_round(q, 3))
-            guarded(s - 3, rs_final)
-
-        @pl.when(t == 4 % tiles)
-        def _():
-            guarded(s - 1, lambda q: rs_round(q, 2))
-
-        @pl.when(t == 5 % tiles)
-        def _():
-            guarded(s - 2, lambda q: rs_round(q, 4))
+
+    spread = 7 if tiles <= 5 else 8
+    plan = [('exch', 0, rs_exchange)]
+    for t, off in ((1, 1), (2, 4), (3, spread), (4, spread + 3)):
+        plan.append((f'r{t}', off, functools.partial(rs_round, t=t)))
+    plan.append(('fin', spread + 6, rs_final))
+
+    def comm(n):
+        for name, off, fn in plan:
+            back = n - off
+
+            @pl.when(jnp.logical_and(back >= tiles, back % tiles == 0))
+            def _(name=name, fn=fn, back=back):
+                with jax.named_scope(name):
+                    q = back // tiles - 1
+
+                    @pl.when(q < n_slice)
+                    def _():
+                        fn(q)
 
     def gather(n):
-        half = n // 2
-        q2 = 2 * HEAD + (half - 4) // 4
-        t2 = (half + 4) % 4 + 1
-
-        @pl.when(n == 0)
-        def _():
-            for q in range(HEAD, 2 * HEAD):
-                ag_first(q)
-
-        @pl.when(jnp.logical_and(half >= 1, half <= 3))
-        def _():
-            for q in range(HEAD, 2 * HEAD):
-                ag_mid(q, half + 1)
-
-        @pl.when(half == 4)
-        def _():
-            for q in range(HEAD, 2 * HEAD):
-                ag_last(q)
-
-        @pl.when(jnp.logical_and(half >= 4, q2 < n_slice))
-        def _():
-            @pl.when(t2 == 1)
-            def _():
-                ag_first(q2)
-
-            @pl.when(t2 > 1)
-            def _():
-                ag_mid(q2, t2)
-
-        @pl.when(jnp.logical_and(jnp.logical_and(half >= 8, t2 == 1), q2 <= n_slice))
-        def _():
-            ag_last(q2 - 1)
+        for tick in range(LONG + 2, LONG + 1 + HEAD):
+            @pl.when(n == 2 * (tick - LONG - 2))
+            def _(tick=tick):
+                for q in range(HEAD):
+                    if tick - q <= LONG + 1:
+                        ag_step(q, tick - q)
+
+        for t in range(1, LONG + 2):
+            @pl.when(n == 2 * (t - 1))
+            def _(t=t):
+                for q in range(HEAD, 2 * HEAD):
+                    ag_step(q, t)
+
+            off = n - 2 * LONG - 2 * (t - 1)
+            q = 2 * HEAD + off // (tiles + 2)
+
+            @pl.when(jnp.logical_and(off >= 0, jnp.logical_and(off % (tiles + 2) == 0, q < n_slice)))
+            def _(t=t, q=q):
+                ag_step(q, t)
 
     def main(n, carry):
         s = n // tiles
@@ -275,7 +268,8 @@
 
         @pl.when(t == 0)
         def _():
-            ag_finish(s)
+            with jax.named_scope('agfin'):
+                ag_finish(s)
             up_t[...] = wts[s, :, 0:rows_dev, :].reshape(width, n_dev * per_dev).T
             for b in range(n_blk):
                 lo = rows_dev + b * per_dev
@@ -296,24 +290,38 @@
                 acc[s % 4, 1, d * per_dev:(d + 1) * per_dev, b * n_dev * per_dev:(b + 1) * n_dev * per_dev] += (
                     g_in[lo:lo + per_dev])
 
-        @pl.when(n % 2 == 0)
-        def _():
+        with jax.named_scope('gath'):
             gather(n)
-        comm(s, t)
+        comm(n)
         return carry
 
     lax.fori_loop(0, n_slice * tiles, main, 0)
 
     def tail(n, carry):
-        comm(n // tiles, n % tiles)
+        comm(n)
         return carry
 
-    lax.fori_loop(n_slice * tiles, (n_slice + 2) * tiles + 3, tail, 0)
+    lax.fori_loop(n_slice * tiles, n_slice * tiles + spread + 7, tail, 0)
     for q in range(n_slice - 3, n_slice):
         send_fin(q).wait_recv()
-    done = pltpu.make_async_copy(fin, out_hbm, load_sem.at[0])
-    done.start()
-    done.wait()
+        send_fin(q).wait_send()
+    done_out = pltpu.make_async_copy(fin.at[0], gout_hbm, load_sem.at[0])
+    done_out.start()
+    with jax.named_scope('perm'):
+        run = n_slice * per_dev
+        group = 128 // per_dev if n_dev * run % 128 == 0 and 128 % per_dev == 0 else 1
+        for b in range(n_blk):
+            for c in range(n_dev * n_slice // group):
+                parts = []
+                for k in range(group):
+                    d, q = divmod(c * group + k, n_slice)
+                    parts.append(fin[1, q, :, b * sl + d * per_dev:b * sl + (d + 1) * per_dev])
+                gin[b * per_dev:(b + 1) * per_dev, c * group * per_dev:(c + 1) * group * per_dev] = (
+                    jnp.concatenate(parts, axis=1))
+    done_in = pltpu.make_async_copy(gin, gin_hbm, load_sem.at[1])
+    done_in.start()
+    done_out.wait()
+    done_in.wait()
 
 
 def SLICE_OF(cfg):
@@ -328,8 +336,7 @@
     tiles = micro // LANES
     cfg = (n_slice, n_dev, micro, toks, width, tiles)
     up = w_in.reshape(rows_dev, n_dev, n_slice, per_dev).transpose(2, 0, 1, 3).reshape(n_slice, rows_dev, sl)
-    down = w_out.reshape(n_slice, per_dev, n_blk, sl).transpose(0, 2, 1, 3).reshape(n_slice, rows_dev, sl)
-    wts = jnp.concatenate([up, down], axis=1)
+    down = w_out.reshape(n_slice, per_dev, width)
     hbm = pl.BlockSpec(memory_space=pl.ANY)
     dma = pltpu.SemaphoreType.DMA
     chunk = 2 * per_dev
@@ -337,9 +344,9 @@
     out = pl.pallas_call(
         functools.partial(step_kernel, cfg),
         name='mlp_grads',
-        out_shape=jax.ShapeDtypeStruct((2, n_slice, per_dev, width), F32),
-        in_specs=[hbm, hbm, pl.BlockSpec(memory_space=pltpu.SMEM), hbm],
-        out_specs=hbm,
+        out_shape=(jax.ShapeDtypeStruct((rows_dev, hidden), F32), jax.ShapeDtypeStruct((n_slice, per_dev, width), F32)),
+        in_specs=[hbm, hbm, pl.BlockSpec(memory_space=pltpu.SMEM), hbm, hbm],
+        out_specs=(hbm, hbm),
         scratch_shapes=[
             pltpu.VMEM((tiles, width, tok), BF16),
             pltpu.VMEM((tiles, tok, width), BF16),
@@ -354,17 +361,16 @@
             pltpu.VMEM((3, LONG + SHORT, chunk, width), F32),
             pltpu.VMEM((3, LONG + SHORT + 1, chunk, width), F32),
             pltpu.VMEM((2, n_slice, per_dev, width), F32),
-            dma((2 * micro + 1,)),
+            pltpu.VMEM((rows_dev, hidden), F32),
+            dma((2 * micro + 1 + n_blk,)),
             dma((n_slice, LONG)), dma((n_slice, LONG)), dma((n_slice, SHORT)), dma((n_slice, SHORT)),
             dma((n_slice, LONG + SHORT + 1)), dma((n_slice, LONG + SHORT + 1)),
             dma((3,)), dma((3,)), dma((3, LONG)), dma((3, LONG)), dma((3, SHORT)), dma((3, SHORT)),
             dma((n_slice,)), dma((n_slice,)),
         ],
         compiler_params=pltpu.CompilerParams(collective_id=0, has_side_effects=True, vmem_limit_bytes=62 * 2 ** 20),
-    )(act, cot, lengths, wts)
-    grad_out = out[0].reshape(n_slice * per_dev, width)
-    grad_in = out[1].reshape(n_slice, per_dev, n_blk, n_dev, per_dev).transpose(2, 1, 3, 0, 4)
-    return grad_in.reshape(rows_dev, hidden), grad_out
+    )(act, cot, lengths.reshape(micro), up, down)
+    return out[0], out[1].reshape(n_slice * per_dev, width)
 
 
 def solution(mesh):

time: 235 us -> 221 us (0.940)
  local copies, waits for them, and re-layouts: 21.6 us -> 6.32 us
    another operation x4 -> x0, local copies, waits for them, and re-layouts: 17.2 us -> none  [the longest x2 10.8 us: run_step(): out[1].reshape(n_slice, per_dev, n_blk, n_dev, per_dev)]
    unnamed x4 -> x3, local copies, waits for them, and re-layouts: 1.76 us -> 5.17 us
where the time goes in v2:
time: 221 us
  Pallas kernels  214 us (97%)
  local copies, waits for them, and re-layouts  6.32 us (3%)
    pallas_call x1, Pallas kernels, run_step(): pl.pallas_call(functools.partial(step_kernel, cfg), name='mlp_grads', out...  214 us
    unnamed x3, local copies, waits for them, and re-layouts  5.17 us

profile of v2, /device:TPU:21, one launch (start us, length us, event | category | flops | bytes accessed | tf_op | source)
XLA Modules:
  0.0 220.9 jit_solution(200683675849252558)
XLA Ops:
  0.6 1.3 copy.8
  2.0 0.2 copy.9
  2.2 1.0 copy.10.up_hbm
  3.1 213.9 %mlp_grads.1 = (f32[48,3072]{1,0:T(8,128)}, f32[12,16,768]{2,1,0:T(8,128)}) custom-call(bf16[12,512,768]{2,1,0:T(8,128)(2,1)} %act_hbm.1, bf16[12,512,768]{2,1,0:T(8,128)(2,1)} %cot_hbm.1, s32[12]{0:T(128)} %bitcast.13, bf16[12,48,256]{2,1,0:T(8,128)(2,1)} %copy.10.up_hbm, bf16[12,16,768]{2,1,0:T(8,128)(2,1)} %bitcast.12), custom_call_target="tpu_custom_call" | custom-call | tf_op jit(solution)/shard_map/mlp_grads/pallas_call | solution.py:344
  217.1 1.9 copy.13
  219.0 1.9 copy.14

commit v3 on v2

v3 whole, which is shorter than its diff:
```python
import functools
import math
import jax
import jax.numpy as jnp
from jax import lax
from jax.experimental import pallas as pl
from jax.experimental.pallas import tpu as pltpu
from jax.sharding import PartitionSpec as P

SQRT_HALF = math.sqrt(0.5)
INV_SQRT_TAU = 1.0 / math.sqrt(2.0 * math.pi)
F32 = jnp.float32
BF16 = jnp.bfloat16
MESH = pl.DeviceIdType.MESH
NT_DIMS = (((1,), (1,)), ((), ()))

SLICE = 256
LANES = 2
HEAD = 3
LONG, SHORT = 4, 3


def gelu_pair(pre_act):
    cdf = 0.5 * (1.0 + lax.erf(pre_act * SQRT_HALF))
    return pre_act * cdf, cdf + pre_act * jnp.exp(-0.5 * pre_act * pre_act) * INV_SQRT_TAU


def dot_nt(left, right):
    return lax.dot_general(left, right, NT_DIMS, preferred_element_type=F32)


def dot_nn(left, right):
    return jnp.dot(left, right, preferred_element_type=F32)


def step_kernel(cfg, act_hbm, cot_hbm, len_smem, up_hbm, down_hbm, fin_hbm,
                act_t, cot, stage, wts, up_t, down, acc, post_s, dpre_s,
                peer, ring_in, ring_out, fin,
                load_sem, agl_s, agl_r, ags_s, ags_r, agx_s, agx_r,
                ex_s, ex_r, rl_s, rl_r, rs_s, rs_r, fin_s, fin_r):
    n_slice, n_dev, micro, toks, width, tiles = cfg
    n_chip = n_dev // 2
    per_dev = SLICE_OF(cfg) // n_dev
    n_blk = width // SLICE_OF(cfg)
    rows_dev = width // n_dev
    chunk = 2 * per_dev
    dev = lax.axis_index('fsdp')
    chip = dev // 2
    core = dev % 2
    sgn = 1 - 2 * core

    def at_chip(off):
        return (chip + sgn * off + 2 * n_chip) % n_chip

    nxt = at_chip(1) * 2 + core
    prv = at_chip(-1) * 2 + core
    sib = chip * 2 + 1 - core

    def remote(src, dst, send, recv, target):
        return pltpu.make_async_remote_copy(src_ref=src, dst_ref=dst, send_sem=send, recv_sem=recv,
                                            device_id={'fsdp': target}, device_id_type=MESH)

    barrier = pltpu.get_barrier_semaphore()
    for other in (nxt, prv, sib):
        pl.semaphore_signal(barrier, inc=1, device_id={'fsdp': other}, device_id_type=MESH)

    sl = n_dev * per_dev
    own_loads = [pltpu.make_async_copy(up_hbm, wts.at[:, dev, pl.ds(0, rows_dev)], load_sem.at[2 * micro])]
    for b in range(n_blk):
        own_loads.append(pltpu.make_async_copy(down_hbm.at[:, :, pl.ds(b * sl, sl)],
                                               wts.at[:, dev, pl.ds(rows_dev + b * per_dev, per_dev)],
                                               load_sem.at[2 * micro + 1 + b]))
    for copy in own_loads:
        copy.start()

    def act_load(k):
        return pltpu.make_async_copy(act_hbm.at[k], stage.at[k % 4], load_sem.at[k])

    def cot_load(k):
        return pltpu.make_async_copy(cot_hbm.at[k], cot.at[k // LANES, pl.ds((k % LANES) * toks, toks)],
                                     load_sem.at[micro + k])

    for k in range(4):
        act_load(k).start()
        cot_load(k).start()
    for copy in own_loads:
        copy.wait()
    pl.semaphore_wait(barrier, 3)

    def piece(q, off):
        return wts.at[q, at_chip(off) * 2 + core]

    def ag_long(q, t):
        ref = piece(q, 1 - t)
        return remote(ref, ref, agl_s.at[q, t - 1], agl_r.at[q, t - 1], nxt)

    def ag_short(q, t):
        ref = piece(q, t - 1)
        return remote(ref, ref, ags_s.at[q, t - 1], ags_r.at[q, t - 1], prv)

    def ag_sib(q, idx, off):
        ref = piece(q, off)
        return remote(ref, ref, agx_s.at[q, idx], agx_r.at[q, idx], sib)

    def ag_first(q):
        ag_long(q, 1).start()
        ag_short(q, 1).start()
        ag_sib(q, 0, 0).start()

    def ag_mid(q, t):
        ag_long(q, t - 1).wait_recv()
        ag_long(q, t).start()
        ag_sib(q, t - 1, 1 - t).start()
        ag_short(q, t - 1).wait_recv()

        if t <= SHORT:
            ag_short(q, t).start()
        ag_sib(q, LONG + t - 1, t - 1).start()

    def ag_last(q):
        ag_long(q, LONG).wait_recv()
        ag_sib(q, LONG, -LONG).start()

    def ag_finish(q):
        for idx in range(LONG + SHORT + 1):
            ag_sib(q, idx, 0).wait_recv()
        for idx in range(LONG + SHORT + 1):
            ag_sib(q, idx, 0).wait_send()
        for t in range(1, LONG + 1):
            ag_long(q, t).wait_send()
        for t in range(1, SHORT + 1):
            ag_short(q, t).wait_send()

    def load_tile(k):
        act_load(k).wait()
        act_t[k // LANES, :, (k % LANES) * toks:(k % LANES + 1) * toks] = stage[k % 4].T
        cot_load(k).wait()
        row = lax.broadcasted_iota(jnp.int32, (toks, 1), 0)
        rows = pl.ds((k % LANES) * toks, toks)
        val = cot[k // LANES, rows, :]
        cot[k // LANES, rows, :] = jnp.where(row < len_smem[k], val, jnp.zeros_like(val))
        if k + 4 < micro:
            act_load(k + 4).start()
            cot_load(k + 4).start()

    def ag_step(q, t):
        if t == 1:
            ag_first(q)
        elif t <= LONG:
            ag_mid(q, t)
        else:
            ag_last(q)

    ag_step(0, 1)
    per_tick = micro // LONG
    for tick in range(2, LONG + 2):
        for k in range((tick - 2) * per_tick, (tick - 1) * per_tick):
            load_tile(k)
        for q in range(HEAD):
            if tick - q >= 1:
                ag_step(q, tick - q)

    need = (4, -3, 3, -2, 2, -1, 1, 0)

    def rows_at(off):
        return pl.ds(pl.multiple_of(at_chip(off) * chunk, chunk), chunk)

    def half_at(off, h):
        return pl.ds(pl.multiple_of(at_chip(off) * chunk + h * per_dev, per_dev), per_dev)

    def exchange(q, off):
        i = need.index(off)
        return remote(acc.at[q % 4, 1 - core, rows_at(-off)], peer.at[q % 3, rows_at(-off)],
                      ex_s.at[q % 3, i], ex_r.at[q % 3, i], sib)

    def send_long(q, t, h):
        return remote(ring_out.at[q % 3, t - 1, h], ring_in.at[q % 3, t - 1, h],
                      rl_s.at[q % 3, t - 1, h], rl_r.at[q % 3, t - 1, h], nxt)

    def send_short(q, t, h):
        return remote(ring_out.at[q % 3, LONG + t - 1, h], ring_in.at[q % 3, LONG + t - 1, h],
                      rs_s.at[q % 3, t - 1, h], rs_r.at[q % 3, t - 1, h], prv)

    def own_sum(q, off, h):
        rows = half_at(off, h)
        return acc[q % 4, core, rows, :] + peer[q % 3, rows, :]

    def send_fin(q):
        return remote(ring_out.at[q % 3, LONG + SHORT, 1 - core], fin.at[core, q], fin_s.at[q], fin_r.at[q], sib)

    def rs_exchange(q):
        def settle():
            send_fin(q - 3).wait_recv()
            send_fin(q - 3).wait_send()
        if isinstance(q, int):
            if q >= 3:
                settle()
        else:
            pl.when(q >= 3)(settle)
        for off in need:
            exchange(q, off).start()

    def rs_round(q, t):
        exchange(q, 5 - t).wait_recv()
        if t <= SHORT:
            exchange(q, t - 4).wait_recv()
        for h in (core, 1 - core):
            val = own_sum(q, 5 - t, h)
            if t > 1:
                send_long(q, t - 1, h).wait_recv()
                val = val + ring_in[q % 3, t - 2, h]
            ring_out[q % 3, t - 1, h] = val
            if t <= SHORT:
                val = own_sum(q, t - 4, h)
                if t > 1:
                    send_short(q, t - 1, h).wait_recv()
                    val = val + ring_in[q % 3, LONG + t - 2, h]
                ring_out[q % 3, LONG + t - 1, h] = val
            send_long(q, t, h).start()
            if t <= SHORT:
                send_short(q, t, h).start()

    def rs_final(q):
        exchange(q, 0).wait_recv()
        for h in (core, 1 - core):
            val = own_sum(q, 0, h)
            send_long(q, LONG, h).wait_recv()
            send_short(q, SHORT, h).wait_recv()
            ring_out[q % 3, LONG + SHORT, h] = val + ring_in[q % 3, LONG - 1, h] + ring_in[q % 3, LONG + SHORT - 1, h]
        send_fin(q).start()
        fin[core, q] = ring_out[q % 3, LONG + SHORT, core]
        for off in need:
            exchange(q, off).wait_send()
        for h in range(2):
            for t in range(1, LONG + 1):
                send_long(q, t, h).wait_send()
            for t in range(1, SHORT + 1):
                send_short(q, t, h).wait_send()

    plan = [(0, rs_exchange)]
    for t, off in ((1, 1), (2, 4), (3, 8), (4, 11)):
        plan.append((off, functools.partial(rs_round, t=t)))
    plan.append((14, rs_final))

    def gather(s, t):
        if t in (0, 2):
            @pl.when(s == 0)
            def _():
                for q in range(HEAD):
                    if LONG + 2 + t // 2 - q <= LONG + 1:
                        ag_step(q, LONG + 2 + t // 2 - q)
        if t in (0, 2, 4):
            @pl.when(s == 0)
            def _():
                for q in range(HEAD, 2 * HEAD):
                    ag_step(q, t // 2 + 1)
        if t in (0, 2):
            @pl.when(s == 1)
            def _():
                for q in range(HEAD, 2 * HEAD):
                    ag_step(q, t // 2 + LONG)
        if t in (1, 3, 5):
            q = s + 2 * HEAD - 1

            @pl.when(jnp.logical_and(s >= 1, q < n_slice))
            def _():
                ag_step(q, t // 2 + 1)
        if t in (1, 3):
            q_old = s + 2 * HEAD - 2

            @pl.when(jnp.logical_and(s >= 2, q_old < n_slice))
            def _():
                ag_step(q_old, t // 2 + LONG)

    def main(s, carry):
        ag_finish(s)
        up_t[...] = wts[s, :, 0:rows_dev, :].reshape(width, sl).T
        for b in range(n_blk):
            lo = rows_dev + b * per_dev
            down[:, b * sl:(b + 1) * sl] = wts[s, :, lo:lo + per_dev, :].reshape(sl, sl)
        acc[s % 4] = jnp.zeros((2, sl, width), F32)
        for t in range(tiles):
            pre = dot_nn(up_t[...], act_t[t]).astype(BF16).astype(F32)
            post, slope = gelu_pair(pre)
            d_act = dot_nt(down[...], cot[t])
            post_s[...] = post.astype(BF16)
            dpre_s[...] = (d_act * slope).astype(BF16)
            acc[s % 4, 0] += dot_nn(post_s[...], cot[t])
            g_in = dot_nt(act_t[t], dpre_s[...])
            for d in range(n_dev):
                for b in range(n_blk):
                    lo = d * rows_dev + b * per_dev
                    acc[s % 4, 1, d * per_dev:(d + 1) * per_dev, b * sl:(b + 1) * sl] += g_in[lo:lo + per_dev]
            gather(s, t)
            for off, fn in plan:
                if off % tiles == t:
                    q = s - 1 - off // tiles

                    @pl.when(q >= 0)
                    def _(q=q, fn=fn):
                        fn(q)
        return carry

    lax.fori_loop(0, n_slice, main, 0)
    for n in range(n_slice * tiles, n_slice * tiles + 15):
        for off, fn in plan:
            q = (n - off) // tiles - 1
            if (n - off) % tiles == 0 and q < n_slice:
                fn(q)
    for q in range(n_slice - 3, n_slice):
        send_fin(q).wait_recv()
        send_fin(q).wait_send()
    done = pltpu.make_async_copy(fin, fin_hbm, load_sem.at[0])
    done.start()
    done.wait()


def order_kernel(dims, fin_hbm, gin_hbm, gout_hbm, fin_out, fin_in, gin, sem):
    n_slice, n_dev, per_dev, n_blk, sl = dims
    get_in = pltpu.make_async_copy(fin_hbm.at[1], fin_in, sem.at[0])
    get_out = pltpu.make_async_copy(fin_hbm.at[0], fin_out, sem.at[1])
    put_out = pltpu.make_async_copy(fin_out, gout_hbm, sem.at[2])
    get_in.start()
    get_out.start()
    get_in.wait()
    group = 128 // per_dev if n_dev * n_slice * per_dev % 128 == 0 and 128 % per_dev == 0 else 1
    for b in range(n_blk):
        for c in range(n_dev * n_slice // group):
            parts = []
            for k in range(group):
                d, q = divmod(c * group + k, n_slice)
                parts.append(fin_in[q, :, b * sl + d * per_dev:b * sl + (d + 1) * per_dev])
            gin[b * per_dev:(b + 1) * per_dev, c * group * per_dev:(c + 1) * group * per_dev] = jnp.concatenate(parts, axis=1)
        if b == 0:
            get_out.wait()
            put_out.start()
    put_in = pltpu.make_async_copy(gin, gin_hbm, sem.at[3])
    put_in.start()
    put_out.wait()
    put_in.wait()


def SLICE_OF(cfg):
    return min(SLICE, cfg[4] // 3)


def run_step(n_dev, act, cot, lengths, w_in, w_out):
    micro, toks, width = act.shape
    hidden = w_in.shape[1]
    sl = min(SLICE, width // 3)
    n_slice, per_dev, n_blk, rows_dev = hidden // sl, sl // n_dev, width // sl, width // n_dev
    tiles = micro // LANES
    cfg = (n_slice, n_dev, micro, toks, width, tiles)
    up = w_in.reshape(rows_dev, n_dev, n_slice, per_dev).transpose(2, 0, 1, 3).reshape(n_slice, rows_dev, sl)
    down = w_out.reshape(n_slice, per_dev, width)
    hbm = pl.BlockSpec(memory_space=pl.ANY)
    dma = pltpu.SemaphoreType.DMA
    tok = toks * LANES
    out = pl.pallas_call(
        functools.partial(step_kernel, cfg),
        name='mlp_grads',
        out_shape=jax.ShapeDtypeStruct((2, n_slice, per_dev, width), F32),
        in_specs=[hbm, hbm, pl.BlockSpec(memory_space=pltpu.SMEM), hbm, hbm],
        out_specs=hbm,
        scratch_shapes=[
            pltpu.VMEM((tiles, width, tok), BF16),
            pltpu.VMEM((tiles, tok, width), BF16),
            pltpu.VMEM((4, toks, width), BF16),
            pltpu.VMEM((n_slice, n_dev, 2 * rows_dev, sl), BF16),
            pltpu.VMEM((sl, width), BF16),
            pltpu.VMEM((sl, width), BF16),
            pltpu.VMEM((4, 2, sl, width), F32),
            pltpu.VMEM((sl, tok), BF16),
            pltpu.VMEM((sl, tok), BF16),
            pltpu.VMEM((3, sl, width), F32),
            pltpu.VMEM((3, LONG + SHORT, 2, per_dev, width), F32),
            pltpu.VMEM((3, LONG + SHORT + 1, 2, per_dev, width), F32),
            pltpu.VMEM((2, n_slice, per_dev, width), F32),
            dma((2 * micro + 1 + n_blk,)),
            dma((n_slice, LONG)), dma((n_slice, LONG)), dma((n_slice, SHORT)), dma((n_slice, SHORT)),
            dma((n_slice, LONG + SHORT + 1)), dma((n_slice, LONG + SHORT + 1)),
            dma((3, 8)), dma((3, 8)), dma((3, LONG, 2)), dma((3, LONG, 2)), dma((3, SHORT, 2)), dma((3, SHORT, 2)),
            dma((n_slice,)), dma((n_slice,)),
        ],
        compiler_params=pltpu.CompilerParams(collective_id=0, has_side_effects=True, vmem_limit_bytes=62 * 2 ** 20),
    )(act, cot, lengths.reshape(micro), up, down)
    grad_in, grad_out = pl.pallas_call(
        functools.partial(order_kernel, (n_slice, n_dev, per_dev, n_blk, sl)),
        name='order_columns',
        out_shape=(jax.ShapeDtypeStruct((rows_dev, hidden), F32), jax.ShapeDtypeStruct((n_slice, per_dev, width), F32)),
        in_specs=[hbm],
        out_specs=(hbm, hbm),
        scratch_shapes=[
            pltpu.VMEM((n_slice, per_dev, width), F32),
            pltpu.VMEM((n_slice, per_dev, width), F32),
            pltpu.VMEM((rows_dev, hidden), F32),
            dma((4,)),
        ],
    )(out)
    return grad_in, grad_out.reshape(n_slice * per_dev, width)


def solution(mesh):
    n_dev = mesh.shape['fsdp']
    shard_spec = P(None, ('rep', 'fsdp'), None)
    len_spec = P(None, ('rep', 'fsdp'))
    weight_spec = P(None, 'fsdp', None)

    def local_step(act_in, cot_out, lengths, w_in, w_out):
        grad_in, grad_out = run_step(n_dev, act_in, cot_out, lengths, w_in[0], w_out[0])
        return grad_in[None], grad_out[None]

    return jax.shard_map(local_step, mesh=mesh, in_specs=(shard_spec, shard_spec, len_spec, weight_spec, weight_spec),
                         out_specs=(shard_spec, shard_spec), check_vma=False)
```

time: 221 us -> 227 us (1.027)
  Pallas kernels: 214 us -> 224 us
  local copies, waits for them, and re-layouts: 6.32 us -> 2.49 us
    pallas_call x1, Pallas kernels: 214 us -> 220 us  [run_step(): pl.pallas_call(functools.partial(step_kernel, cfg), name='mlp_grads', out...]
    unnamed x3 -> x1, local copies, waits for them, and re-layouts: 5.17 us -> 1.33 us
    pallas_call x0 -> x1, Pallas kernels: none -> 3.11 us  [run_step(): pl.pallas_call(functools.partial(order_kernel, (n_slice, n_dev, per_dev,...]
where the time goes in v3:
time: 227 us
  Pallas kernels  224 us (99%)
  local copies, waits for them, and re-layouts  2.49 us (1%)
    pallas_call x1, Pallas kernels, run_step(): pl.pallas_call(functools.partial(step_kernel, cfg), name='mlp_grads', out...  220 us

profile of v3, /device:TPU:21, one launch (start us, length us, event | category | flops | bytes accessed | tf_op | source)
XLA Modules:
  0.0 226.9 jit_solution(10874591049715698724)
XLA Ops:
  0.6 1.3 copy.8
  2.0 0.2 copy.9
  2.2 1.0 copy.10.up_hbm
  3.1 220.4 %mlp_grads.1.fin_hbm = f32[2,12,16,768]{3,2,1,0:T(8,128)} custom-call(bf16[12,512,768]{2,1,0:T(8,128)(2,1)} %act_hbm.1, bf16[12,512,768]{2,1,0:T(8,128)(2,1)} %cot_hbm.1, s32[12]{0:T(128)} %bitcast.11, bf16[12,48,256]{2,1,0:T(8,128)(2,1)} %copy.10.up_hbm, bf16[12,16,768]{2,1,0:T(8,128)(2,1)} %bitcast.10), custom_call_target="tpu_custom_call" | custom-call | tf_op jit(solution)/shard_map/mlp_grads/pallas_call | solution.py:359
  223.6 3.1 %order_columns.1 = (f32[48,3072]{1,0:T(8,128)}, f32[12,16,768]{2,1,0:T(8,128)}) custom-call(f32[2,12,16,768]{3,2,1,0:T(8,128)} %mlp_grads.1.fin_hbm), custom_call_target="tpu_custom_call" | custom-call | tf_op jit(solution)/shard_map/order_columns/pallas_call | solution.py:387
